TPU v7x, 256 devices: a whole 4x4x8 slice. The times are simulated.
256 devices in a mesh: row: 16 (over x_hi, z), col: 16 (over x_lo, y, core).
Axes of the slice: x: 4 (x_hi: 2, x_lo: 2; x = x_hi * 2 + x_lo), y: 4, z: 8, core: 2. Of those that a mesh axis runs over, the one named last changes fastest.
Arguments:
- queries: bfloat16 [32768, 768], P(('row', 'col')), may hold values from -6 to 6
- keys: bfloat16 [32768, 768], P(('row', 'col')), may hold values from -6 to 6
- values: bfloat16 [32768, 768], P(('row', 'col')), may hold values from -6 to 6
- query_gain: float32 [128], replicated, may hold values from 0.8 to 3
- key_gain: float32 [128], replicated, may hold values from 0.8 to 3
Outputs:
- attended: bfloat16 [32768, 768], P(('row', 'col'))
All inputs are finite; a program needn't handle non-finite values.
Results may differ from a plain program's by a relative error of at most 0.011.
Values may be sent and summed in bfloat16 or wider, within the bound.
No kernel may reach another device: no remote copies, remote signals or barrier semaphores. Data moves between devices by JAX's collectives and lax.ppermute only.
A program may use at most 64 MiB of HBM per device.

v0:
```python
import math

import jax
import jax.numpy as jnp
from jax import lax
from jax.sharding import Mesh
from jax.sharding import PartitionSpec as P

HEADS = 6
DH = 128
COL = ("col_0", "col_1", "col_2")
ROW_COL = ("row", "col_0", "col_1", "col_2")


EPSILON = 0.1


def from_everyone(x, axis):
    devices = lax.axis_size(axis)
    return lax.all_to_all(jnp.broadcast_to(x[None], (devices, *x.shape)), axis, 0, 0, tiled=True)


def joined_along(parts, dim):
    dims = list(parts.shape[1:])
    dims[dim] *= parts.shape[0]
    return jnp.moveaxis(parts, 0, dim).reshape(dims)


def gather_axes(x, axes, dim):
    far, near = axes
    leading = from_everyone(x, far)
    parts = jnp.swapaxes(from_everyone(leading, near), 0, 1)
    return joined_along(parts.reshape(-1, *x.shape), dim)


def sent_together(arrays, axis, dim, along):
    both = jnp.concatenate(arrays, axis=along)
    filled, at, finished = (lax.all_gather(both, axis, axis=dim, tiled=True), 0, [])
    for a in arrays:
        finished.append(lax.slice_in_dim(filled, at, at + a.shape[along], axis=along))
        at += a.shape[along]
    return tuple(finished)


def in_blocks(x, dim, devices):
    before, after = (x.shape[:dim], x.shape[dim + 1 :])
    return jnp.moveaxis(x.reshape(*before, devices, -1, *after), dim, 0)


def sent_and_summed(x, axis, dim):
    devices = lax.axis_size(axis)
    parts = lax.all_to_all(in_blocks(x, dim, devices), axis, 0, 0, tiled=True)
    return jnp.sum(parts.astype(jnp.float32), axis=0)


def sum_by_axis(x, axes, dim):
    far, near = axes
    parts = in_blocks(x, dim, lax.axis_size(far))
    nearer = sent_and_summed(parts, near, dim + 1)
    arrived = lax.all_to_all(
        nearer.astype(jnp.bfloat16), far, split_axis=0, concat_axis=0, tiled=True
    )
    return arrived.astype(jnp.float32).sum(axis=0)


def normed(entries, gain):
    rows = entries.shape[0]
    shaped = entries.reshape(rows, HEADS, DH).astype(jnp.float32)
    inverse = lax.rsqrt(jnp.mean(shaped * shaped, axis=-1, keepdims=True) + EPSILON)
    return (shaped * inverse * gain).astype(jnp.bfloat16).reshape(rows, HEADS * DH)


def attend(query_rows, key_block, value_block, shift):
    count = query_rows.shape[0]
    block = math.gcd(count, 512)
    query_blocks = query_rows.reshape(count // block, block, HEADS, DH)
    key_rows = key_block.reshape(key_block.shape[0], HEADS, DH)
    value_rows = value_block.reshape(value_block.shape[0], HEADS, DH)
    inverse_root = 1.0 / math.sqrt(DH)

    def one_block(query_block):
        scores = (
            jnp.einsum("qhd,khd->hqk", query_block, key_rows, preferred_element_type=jnp.float32)
            * inverse_root
        )
        weights = jax.nn.sigmoid(scores - shift).astype(jnp.bfloat16)
        mixed = jnp.einsum("hqk,khd->qhd", weights, value_rows, preferred_element_type=jnp.float32)
        return mixed.reshape(block, HEADS * DH)

    return lax.map(one_block, query_blocks).reshape(count, HEADS * DH)


def per_device(queries, keys, values, query_gain, key_gain):
    shift = math.log(queries.shape[0] * lax.axis_size("row") * lax.axis_size(COL))
    query_send = normed(queries, query_gain)
    key_send = normed(keys, key_gain)
    gathered = gather_axes(query_send, (("col_0", "col_1"), "col_2"), 0)
    key_block, value_block = sent_together((key_send, values), "row", 0, 1)
    totals = attend(gathered, key_block, value_block, shift)
    result = sum_by_axis(totals.astype(jnp.bfloat16), (("col_0", "col_1"), "col_2"), 0)
    return result.astype(jnp.bfloat16)


def solution(mesh):
    torus = Mesh(
        mesh.devices.reshape(mesh.shape["row"], 2, 4, 2), ("row", "col_0", "col_1", "col_2")
    )
    return jax.shard_map(
        per_device,
        mesh=torus,
        in_specs=(P(ROW_COL, None), P(ROW_COL, None), P(ROW_COL, None), P(), P()),
        out_specs=P(ROW_COL, None),
        check_vma=False,
    )
```

profile of v0, /device:TPU:32, one launch (start us, length us, event | category | flops | bytes accessed | tf_op | source)
XLA Modules:
  0.0 251.8 jit_solution(11341427326031621734)
XLA Ops:
  6.5 1.1 copy.25
  7.8 1.1 copy.26
  9.1 0.8 pad_maximum_fusion
  10.3 1.3 broadcast_in_dim.26
  11.7 5.4 %all-to-all-start = ((bf16[8,128,768]{1,2,0:T(8,128)(2,1)}), bf16[8,128,768]{1,2,0:T(8,128)(2,1)S(1)}, u32[]{:S(2)}, u32[]{:S(2)}) async-start(bf16[8,128,768]{1,2,0:T(8,128)(2,1)} %broadcast_in_dim.26), calls=%async_computation | async-start | bytes 3145728 | tf_op jit(solution)/shard_map/all_to_all | solution.py:20
  17.1 23.5 %all-to-all-done = bf16[8,128,768]{1,2,0:T(8,128)(2,1)S(1)} async-done(((bf16[8,128,768]{1,2,0:T(8,128)(2,1)}), bf16[8,128,768]{1,2,0:T(8,128)(2,1)S(1)}, u32[]{:S(2)}, u32[]{:S(2)}) %all-to-all-start) | async-done | bytes 1572896 | tf_op jit(solution)/shard_map/all_to_all | solution.py:20
  40.6 1.0 copy.23
  41.8 6.3 %all_to_all.20 = bf16[2,8,128,768]{2,1,3,0:T(8,128)(2,1)S(1)} all-to-all(bf16[2,8,128,768]{2,1,3,0:T(8,128)(2,1)S(1)} %broadcast_in_dim.27), channel_id=1, replica_groups=mesh['row'=16,'col_0'=2,'col_1'=4,'col_2'=2] {'col_2'}, dimensions={0} | all-to-all | bytes 6291456 | tf_op jit(solution)/shard_map/all_to_all | solution.py:20
  48.1 4.9 %copy.24 = bf16[8,2,128,768]{2,1,0,3:T(2,128)(2,1)S(1)} copy(bf16[8,2,128,768]{2,0,3,1:T(8,128)(2,1)S(1)} %bitcast.36) | data formatting | bytes 6291456 | tf_op jit(solution)/shard_map/transpose | solution.py:32
  52.9 3.2 %reshape_reshape_reshape.3 = bf16[4,512,6,128]{1,0,3,2:T(4,128)(2,1)} reshape(bf16[8,2,128,768]{2,1,0,3:T(2,128)(2,1)S(1)} %copy.24) | data formatting | bytes 6291456 | tf_op jit(solution)/shard_map/reshape;reshape;reshape | solution.py:76
  56.2 6.2 %copy.27 = bf16[4,512,6,128]{3,1,2,0:T(8,128)(2,1)} copy(bf16[4,512,6,128]{1,0,3,2:T(4,128)(2,1)} %reshape_reshape_reshape.3) | data formatting | bytes 6291456 | tf_op jit(solution)/shard_map/while | solution.py:90
  62.3 80.9 %all-gather.2.cloned.1.call-done = bf16[2048,1536]{0,1:T(8,128)(2,1)} async-done(((bf16[128,1536]{0,1:T(8,128)(2,1)}), bf16[2048,1536]{0,1:T(8,128)(2,1)}) %all-gather.2.cloned.1.call-update) | async-done | bytes 6291472 | tf_op jit(solution)/shard_map/all_gather | solution.py:38
  143.2 5.3 %fusion.16 = (bf16[2048,768]{0,1:T(8,128)(2,1)}, bf16[2048,768]{0,1:T(8,128)(2,1)S(1)}) fusion(bf16[2048,1536]{0,1:T(8,128)(2,1)} %all-gather.2.cloned.1.call-done), kind=kLoop, calls=%fused_computation.23 | loop fusion | bytes 12582912 | tf_op jit(solution)/shard_map/slice | solution.py:40
  148.5 2.8 %copy.28 = bf16[2048,6,128]{2,0,1:T(8,128)(2,1)} copy(bf16[2048,6,128]{0,2,1:T(8,128)(2,1)S(1)} %bitcast.37) | data formatting | bytes 6291456 | tf_op jit(solution)/shard_map/while | solution.py:90
  151.3 56.2 %while.12 = (s32[]{:T(128)}, bf16[4,512,768]{2,1,0:T(8,128)(2,1)}, bf16[4,512,6,128]{3,1,2,0:T(8,128)(2,1)}, bf16[2048,6,128]{2,0,1:T(8,128)(2,1)}, bf16[2048,6,128]{0,2,1:T(8,128)(2,1)}, /*index=5*/s32[]{:T(128)}) while((s32[]{:T(128)}, bf16[4,512,768]{2,1,0:T(8,128)(2,1)}, bf16[4,512,6,128]{3,1,2,0:T(8,128)(2,1)}, ...), condition=%wide.region_3.4_spmd, body=%wide.region_2.3_spmd.sunk | while | flops 3258974208 | bytes 11011141 | solution.py:90
  151.3 12.8 %fusion.26 = bf16[6,512,128]{1,2,0:T(8,128)(2,1)S(1)} fusion(bf16[2048,6,128]{0,2,1:T(8,128)(2,1)} %get-tuple-element.145, bf16[2048,6,128]{2,0,1:T(8,128)(2,1)} %get-tuple-element.144, bf16[4,512,6,128]{3,1,2,0:T(8,128)(2,1)} %get-tuple-element.143, s32[]{:T(128)} %get-tuple-element.135), kind=kOutput, calls=%fused_computation.1.clone.1 | convolution fusion | flops 3258974208 | bytes 7864832 | tf_op jit(solution)/shard_map/while/body/eval_jaxpr/hqk,khd->qhd/dot_general | solution.py:87
  164.2 0.3 copy.36
  164.5 1.0 constant_dynamic-update-slice_fusion.2
  165.4 12.8 %fusion.26 = bf16[6,512,128]{1,2,0:T(8,128)(2,1)S(1)} fusion(bf16[2048,6,128]{0,2,1:T(8,128)(2,1)} %get-tuple-element.145, bf16[2048,6,128]{2,0,1:T(8,128)(2,1)} %get-tuple-element.144, bf16[4,512,6,128]{3,1,2,0:T(8,128)(2,1)} %get-tuple-element.143, s32[]{:T(128)} %get-tuple-element.135), kind=kOutput, calls=%fused_computation.1.clone.1 | convolution fusion | flops 3258974208 | bytes 7864832 | tf_op jit(solution)/shard_map/while/body/eval_jaxpr/hqk,khd->qhd/dot_general | solution.py:87
  178.3 0.3 copy.36
  178.6 0.9 constant_dynamic-update-slice_fusion.2
  179.5 12.8 %fusion.26 = bf16[6,512,128]{1,2,0:T(8,128)(2,1)S(1)} fusion(bf16[2048,6,128]{0,2,1:T(8,128)(2,1)} %get-tuple-element.145, bf16[2048,6,128]{2,0,1:T(8,128)(2,1)} %get-tuple-element.144, bf16[4,512,6,128]{3,1,2,0:T(8,128)(2,1)} %get-tuple-element.143, s32[]{:T(128)} %get-tuple-element.135), kind=kOutput, calls=%fused_computation.1.clone.1 | convolution fusion | flops 3258974208 | bytes 7864832 | tf_op jit(solution)/shard_map/while/body/eval_jaxpr/hqk,khd->qhd/dot_general | solution.py:87
  192.3 0.3 copy.36
  192.6 0.9 constant_dynamic-update-slice_fusion.2
  193.5 12.8 %fusion.26 = bf16[6,512,128]{1,2,0:T(8,128)(2,1)S(1)} fusion(bf16[2048,6,128]{0,2,1:T(8,128)(2,1)} %get-tuple-element.145, bf16[2048,6,128]{2,0,1:T(8,128)(2,1)} %get-tuple-element.144, bf16[4,512,6,128]{3,1,2,0:T(8,128)(2,1)} %get-tuple-element.143, s32[]{:T(128)} %get-tuple-element.135), kind=kOutput, calls=%fused_computation.1.clone.1 | convolution fusion | flops 3258974208 | bytes 7864832 | tf_op jit(solution)/shard_map/while/body/eval_jaxpr/hqk,khd->qhd/dot_general | solution.py:87
  206.3 0.3 copy.36
  206.6 1.0 constant_dynamic-update-slice_fusion.2
  207.6 2.2 copy.30
  209.7 6.3 %all_to_all.21 = bf16[2,8,128,768]{3,2,1,0:T(8,128)(2,1)S(1)} all-to-all(bf16[2,8,128,768]{3,2,1,0:T(8,128)(2,1)S(1)} %copy.30), channel_id=1, replica_groups=mesh['row'=16,'col_0'=2,'col_1'=4,'col_2'=2] {'col_2'}, dimensions={0} | all-to-all | bytes 6291456 | tf_op jit(solution)/shard_map/all_to_all | solution.py:52
  216.0 2.1 reduce_sum.44
  218.1 25.9 %all_to_all.22 = bf16[8,128,768]{2,1,0:T(8,128)(2,1)S(1)} all-to-all(bf16[8,128,768]{2,1,0:T(8,128)(2,1)} %reduce_sum.44), channel_id=1, replica_groups=mesh['row'=16,'col_0'=2,'col_1'=4,'col_2'=2] {'col_0','col_1'}, dimensions={0} | all-to-all | bytes 3145728 | tf_op jit(solution)/shard_map/all_to_all | solution.py:60
  244.0 0.9 reduce_sum.45
  (21 shorter events, 0.9 us)
Async XLA Ops:
  6.5 1.2 copy-start
  6.5 3.3 %copy-start.1 = (bf16[128,768]{1,0:T(8,128)(2,1)S(1)}, bf16[128,768]{1,0:T(8,128)(2,1)}, u32[]{:S(2)}) copy-start(bf16[128,768]{1,0:T(8,128)(2,1)} %param.7) | copy-start | bytes 589828
  6.5 3.6 %copy-start.2 = (f32[128]{0:T(128)S(1)}, f32[128]{0:T(128)}, u32[]{:S(2)}) copy-start(f32[128]{0:T(128)} %param.10) | copy-start | bytes 1540
  6.5 136.7 %all-gather.2.cloned.1.call-start = ((), (), s32[]{:S(2)}) async-start(), calls=%async_computation.4 | async-start | bytes 6684672 | tf_op jit(solution)/shard_map/all_gather | solution.py:38
  11.7 28.9 %all-to-all-start = ((bf16[8,128,768]{1,2,0:T(8,128)(2,1)}), bf16[8,128,768]{1,2,0:T(8,128)(2,1)S(1)}, u32[]{:S(2)}, u32[]{:S(2)}) async-start(bf16[8,128,768]{1,2,0:T(8,128)(2,1)} %broadcast_in_dim.26), calls=%async_computation | async-start | bytes 3145728 | tf_op jit(solution)/shard_map/all_to_all | solution.py:20
Sparse Core Ops, SparseCore 0:
  10.0 133.1 all-gather.1
where the time goes:
time: 252 us
  waiting for transfers between devices  104 us (41%)
  matrix products  51.3 us (20%)
  blocking collectives  38.4 us (15%)
  local copies, waits for them, and re-layouts  34.4 us (14%)
  between operations  13.5 us (5%)
  starting transfers between devices  5.4 us (2%)
  other arithmetic  4.33 us (2%)
    all_gather x1, waiting for transfers between devices, sent_together(): lax.all_gather(both, axis, axis=dim, tiled=True)  80.9 us
    dot_general x4, matrix products, one_block(): jnp.einsum('hqk,khd->qhd', weights, value_rows, preferred_element_type=jn...  51.3 us
    all_to_all x1, blocking collectives, sum_by_axis(): lax.all_to_all(nearer.astype(jnp.bfloat16), far, split_axis=0, concat_axi...  25.9 us
    all_to_all x1, waiting for transfers between devices, from_everyone(): lax.all_to_all(jnp.broadcast_to(x[None], (devices, *x.shape)), axis, 0, 0...  23.5 us
    while x2, local copies, waits for them, and re-layouts, attend(): return lax.map(one_block, query_blocks).reshape(count, HEADS * DH)  8.98 us
    all_to_all x1, blocking collectives, from_everyone(): lax.all_to_all(jnp.broadcast_to(x[None], (devices, *x.shape)), axis, 0, 0...  6.26 us
    all_to_all x1, blocking collectives, sent_and_summed(): parts = lax.all_to_all(in_blocks(x, dim, devices), axis, 0, 0, tiled=True)  6.26 us
    all_to_all x1, starting transfers between devices, from_everyone(): lax.all_to_all(jnp.broadcast_to(x[None], (devices, *x.shape)), axis, 0, 0...  5.4 us
  transfers between devices with their start and end apart: 2, of which 2 were waited for; matrix products, arithmetic and copies ran while one was open for 7% of the time, Pallas kernels for 0%

commit v1 on v0

v1 whole, which is shorter than its diff:
```python
import functools
import math

import jax
import jax.numpy as jnp
from jax import lax
from jax.experimental import pallas as pl
from jax.experimental.pallas import tpu as pltpu
from jax.sharding import Mesh
from jax.sharding import PartitionSpec as P

AXES = ("xh", "z", "xl", "y", "c")
PLANE = ("xh", "xl", "y")
HEADS = 6
DH = 128
HALF = 3
EPSILON = 0.1
SLOPE = -math.log2(math.e) / math.sqrt(DH)

VM = pl.BlockSpec(memory_space=pltpu.VMEM)
SM = pl.BlockSpec(memory_space=pltpu.SMEM)


def prepare_body(half_ref, q_ref, k_ref, v_ref, qg_ref, kg_ref, qt_ref, mine_ref, other_ref, both):
    half = half_ref[0]

    def normed(ref, gain_ref, h):
        x = ref[:, h * DH : (h + 1) * DH].astype(jnp.float32)
        inverse = lax.rsqrt(jnp.mean(x * x, axis=-1, keepdims=True) + EPSILON)
        return x * inverse * gain_ref[...]

    for h in range(HEADS):
        g, i = h // HALF, h % HALF
        both[g, i] = normed(k_ref, kg_ref, h).astype(jnp.bfloat16)
        v = v_ref[:, h * DH : (h + 1) * DH].astype(jnp.float32)
        both[g, HALF + i] = v.T.astype(jnp.bfloat16)
        qt = normed(q_ref, qg_ref, h).T.astype(jnp.bfloat16)
        for d in range(8):
            qt_ref[g * 8 + d, i] = qt
    mine_ref[...] = both[half]
    other_ref[...] = both[1 - half]


def prepare(half, q, k, v, qg, kg):
    rows = q.shape[0]
    pack = jax.ShapeDtypeStruct((2 * HALF, DH, rows), jnp.bfloat16)
    return pl.pallas_call(
        prepare_body,
        out_shape=(jax.ShapeDtypeStruct((16, HALF, DH, rows), jnp.bfloat16), pack, pack),
        in_specs=[SM] + [VM] * 5,
        out_specs=(VM, VM, VM),
        scratch_shapes=[pltpu.VMEM((2, 2 * HALF, DH, rows), jnp.bfloat16)],
        name="prepare",
    )(half, q, k, v, qg, kg)


def attend_body(tokens, kinds, first, last, *refs):
    n = len(kinds)
    qt, out = refs[0], refs[-1]
    total_in = None if first else refs[1 + n]
    units = []
    for ref, pair in zip(refs[1 : 1 + n], kinds):
        units += [ref.at[0], ref.at[1]] if pair else [ref]
    shift = 1.0 / tokens

    def one(i, _):
        for h in range(HALF):
            q = jnp.concatenate([qt[2 * i, h], qt[2 * i + 1, h]], axis=1)
            total = None
            for a, b in zip(units[::2], units[1::2]):
                k = jnp.concatenate([a[h], b[h]], axis=0)
                vt = jnp.concatenate([a[HALF + h], b[HALF + h]], axis=1)
                s = jnp.dot(k, q, preferred_element_type=jnp.float32)
                u = jnp.exp2(s * SLOPE) + shift
                w = jnp.bfloat16(1.0) / u.astype(jnp.bfloat16)
                o = jnp.dot(vt, w, preferred_element_type=jnp.float32)
                total = o if total is None else total + o
            for j in range(2):
                r = total[:, DH * j : DH * (j + 1)]
                if not first:
                    r = r + total_in[2 * i + j, h]
                out[2 * i + j, h] = (r * shift).astype(jnp.bfloat16) if last else r
        return 0

    lax.fori_loop(0, 8, one, 0)


def attend(tokens, qt, blocks, total, last):
    kinds = tuple(b.ndim == 4 for b in blocks)
    first = total is None
    args = [qt, *blocks] + ([] if first else [total])
    keys = 128 * sum(2 if p else 1 for p in kinds)
    pairs = keys * 2048 * HALF
    return pl.pallas_call(
        functools.partial(attend_body, tokens, kinds, first, last),
        out_shape=jax.ShapeDtypeStruct(qt.shape, jnp.bfloat16 if last else jnp.float32),
        in_specs=[VM] * len(args),
        out_specs=VM,
        input_output_aliases={} if first or last else {len(args) - 1: 0},
        cost_estimate=pl.CostEstimate(
            flops=pairs * DH * 4, bytes_accessed=8 << 20, transcendentals=2 * pairs
        ),
        name=f"attend{keys}",
    )(*args)


def finish_body(parts_ref, out_ref):
    for h in range(HEADS):
        g, i = h // HALF, h % HALF
        total = parts_ref[g * 8, i].astype(jnp.float32)
        for s in range(1, 8):
            total = total + parts_ref[g * 8 + s, i].astype(jnp.float32)
        out_ref[:, h * DH : (h + 1) * DH] = total.T.astype(jnp.bfloat16)


def finish(parts, rows):
    return pl.pallas_call(
        finish_body,
        out_shape=jax.ShapeDtypeStruct((rows, HEADS * DH), jnp.bfloat16),
        in_specs=[VM],
        out_specs=VM,
        name="finish",
    )(parts)


def per_device(queries, keys, values, query_gain, key_gain):
    rows = queries.shape[0]
    tokens = rows * lax.axis_size(AXES)
    half = lax.axis_index("xh").astype(jnp.int32).reshape(1)
    qt_send, mine, other = prepare(
        half, queries, keys, values, query_gain.reshape(1, DH), key_gain.reshape(1, DH)
    )
    partner = [(0, 3), (3, 0), (1, 2), (2, 1)]
    n = lax.axis_size("z")
    up = [(i, (i + 1) % n) for i in range(n)]
    down = [(i, (i - 1) % n) for i in range(n)]
    swap = [(0, 1), (1, 0)]

    theirs = lax.ppermute(other, ("xh", "xl"), partner)
    own = lax.all_to_all(qt_send, PLANE, 0, 0, tiled=True)
    block = jnp.stack([mine, theirs])
    groups = [[block]]
    u = d = block
    for step in range(3):
        u, d = lax.ppermute(u, "z", up), lax.ppermute(d, "z", down)
        groups.append([u, d])
    u, d = lax.ppermute(u[0], "z", up), lax.ppermute(d[1], "z", down)
    groups.append([u, d])
    peer = lax.ppermute(own, "c", swap)

    groups = [groups[0] + groups[1], groups[2], groups[3], groups[4]]
    totals = [None, None]
    for s, group in enumerate(groups):
        last = s == len(groups) - 1
        for who in (1, 0):
            totals[who] = attend(tokens, (own, peer)[who], group, totals[who], last)
    back = lax.ppermute(totals[1], "c", swap)
    parts = (totals[0].astype(jnp.float32) + back.astype(jnp.float32)).astype(jnp.bfloat16)
    parts = lax.all_to_all(parts, PLANE, 0, 0, tiled=True)
    return finish(parts, rows)


def solution(mesh):
    torus = Mesh(mesh.devices.reshape(2, 8, 2, 4, 2), AXES)
    return jax.shard_map(
        per_device,
        mesh=torus,
        in_specs=(P(AXES, None), P(AXES, None), P(AXES, None), P(), P()),
        out_specs=P(AXES, None),
        check_vma=False,
    )
```

time: 252 us -> 210 us (0.83)
  Pallas kernels: 0 us -> 104 us
  waiting for transfers between devices: 104 us -> 50.8 us
  matrix products: 51.3 us -> 0 us
  local copies, waits for them, and re-layouts: 34.4 us -> 3.98 us
  between operations: 13.5 us -> 0.08 us
  starting transfers between devices: 5.4 us -> 18.1 us
  blocking collectives: 38.4 us -> 28 us
    pallas_call x0 -> x10, Pallas kernels: none -> 104 us  [the longest x8 99.1 us: attend(): pl.pallas_call(functools.partial(attend_body, tokens, kinds, first, last)...]
    all_gather x1 -> x0, waiting for transfers between devices: 80.9 us -> none  [sent_together(): lax.all_gather(both, axis, axis=dim, tiled=True)]
    dot_general x4 -> x0, matrix products: 51.3 us -> none  [one_block(): jnp.einsum('hqk,khd->qhd', weights, value_rows, preferred_element_type=jn...]
    ppermute x0 -> x11, waiting for transfers between devices: none -> 50.8 us  [the longest x6 29.5 us: per_device(): u, d = (lax.ppermute(u, 'z', up), lax.ppermute(d, 'z', down))]
    all_to_all x1, waiting for transfers between devices: 23.5 us -> 0.01 us  [per_device(): own = lax.all_to_all(qt_send, PLANE, 0, 0, tiled=True)]
    ppermute x0 -> x11, starting transfers between devices: none -> 10.9 us  [the longest x6 6.65 us: per_device(): u, d = (lax.ppermute(u, 'z', up), lax.ppermute(d, 'z', down))]
    all_to_all x3 -> x1, blocking collectives: 38.4 us -> 28 us  [per_device(): parts = lax.all_to_all(parts, PLANE, 0, 0, tiled=True)]
    while x2 -> x0, local copies, waits for them, and re-layouts: 8.98 us -> none  [attend(): return lax.map(one_block, query_blocks).reshape(count, HEADS * DH)]
  transfers between devices with their start and end apart: 2 -> 12, of which waited for: 2 -> 7; matrix products, arithmetic and copies ran while one was open for 7% -> 1% of each run, Pallas kernels for 0% -> 43%
where the time goes in v1:
time: 210 us; the launch traced here: 207 us
  Pallas kernels  104 us (50%)
  waiting for transfers between devices  50.8 us (24%)
  blocking collectives  28 us (13%)
  starting transfers between devices  18.1 us (9%)
  local copies, waits for them, and re-layouts  3.98 us (2%)
    pallas_call x8, Pallas kernels, attend(): pl.pallas_call(functools.partial(attend_body, tokens, kinds, first, last)...  99.1 us
    ppermute x6, waiting for transfers between devices, per_device(): u, d = (lax.ppermute(u, 'z', up), lax.ppermute(d, 'z', down))  29.5 us
    all_to_all x1, blocking collectives, per_device(): parts = lax.all_to_all(parts, PLANE, 0, 0, tiled=True)  28 us
    ppermute x1, waiting for transfers between devices, per_device(): theirs = lax.ppermute(other, ('xh', 'xl'), partner)  21.3 us
    all_to_all x1, starting transfers between devices, per_device(): own = lax.all_to_all(qt_send, PLANE, 0, 0, tiled=True)  7.17 us
    ppermute x6, starting transfers between devices, per_device(): u, d = (lax.ppermute(u, 'z', up), lax.ppermute(d, 'z', down))  6.65 us
  transfers between devices with their start and end apart: 12, of which 7 were waited for; matrix products, arithmetic and copies ran while one was open for 1% of the time, Pallas kernels for 43%

profile of v1, /device:TPU:32, one launch (start us, length us, event | category | flops | bytes accessed | tf_op | source)
XLA Modules:
  0.0 207.3 jit_solution(15711037566921805521)
XLA Ops:
  0.0 2.9 %prepare.1 = (bf16[16,3,128,128]{3,2,1,0:T(8,128)(2,1)}, bf16[6,128,128]{2,1,0:T(8,128)(2,1)}, bf16[6,128,128]{2,1,0:T(8,128)(2,1)}) custom-call(s32[1]{0:T(128)} %bitcast.half_ref, bf16[128,768]{1,0:T(8,128)(2,1)} %q_ref.1, bf16[128,768]{1,0:T(8,128)(2,1)} %k_ref.1, bf16[128,768]{1,0:T(8,128)(2,1)} %v_ref.1, f32[1,128]{1,0:T(1,128)} %bitcast.11, ...), custom_call_target="tpu_custom_call" | custom-call | tf_op jit(solution)/shard_map/prepare/pallas_call | solution.py:47
  2.9 7.2 %all-to-all-start = ((bf16[16,3,128,128]{3,2,1,0:T(8,128)(2,1)}), bf16[16,3,128,128]{3,2,1,0:T(8,128)(2,1)S(1)}, u32[]{:S(2)}, u32[]{:S(2)}) async-start(bf16[16,3,128,128]{3,2,1,0:T(8,128)(2,1)} %get-tuple-element.8), calls=%async_computation | async-start | bytes 3145728 | tf_op jit(solution)/shard_map/all_to_all | solution.py:140
  10.1 3.2 %collective-permute-start = (bf16[6,128,128]{2,1,0:T(8,128)(2,1)S(1)}, bf16[6,128,128]{2,1,0:T(8,128)(2,1)S(1)}, u32[]{:S(2)}, u32[]{:S(2)}) collective-permute-start(bf16[6,128,128]{2,1,0:T(8,128)(2,1)S(1)} %copy-done.11), channel_id=1, source_target_pairs={{0,136},{136,0},{8,128},{128,8},{1,137},{137,1},{9,129},{129,9},{2... | collective-permute-start | bytes 589832 | tf_op jit(solution)/shard_map/ppermute | solution.py:139
  13.3 21.3 %collective-permute-done = bf16[6,128,128]{2,1,0:T(8,128)(2,1)S(1)} collective-permute-done((bf16[6,128,128]{2,1,0:T(8,128)(2,1)S(1)}, bf16[6,128,128]{2,1,0:T(8,128)(2,1)S(1)}, u32[]{:S(2)}, u32[]{:S(2)}) %collective-permute-start) | collective-permute-done | bytes 196640 | tf_op jit(solution)/shard_map/ppermute | solution.py:139
  34.6 2.0 collective-permute-start.1
  36.6 0.2 collective-permute-start.5
  36.8 7.7 %collective-permute-done.1.refs_2_ = bf16[2,6,128,128]{3,2,1,0:T(8,128)(2,1)} collective-permute-done((bf16[2,6,128,128]{3,2,1,0:T(8,128)(2,1)S(1)}, bf16[2,6,128,128]{3,2,1,0:T(8,128)(2,1)}, u32[]{:S(2)}, u32[]{:S(2)}) %collective-permute-start.1) | collective-permute-done | bytes 393248 | tf_op jit(solution)/shard_map/ppermute | solution.py:145
  44.5 1.9 collective-permute-start.2
  46.5 1.9 collective-permute-done.5.refs_3_
  48.3 1.5 collective-permute-start.6
  49.9 6.5 %collective-permute-done.2.refs_1_ = bf16[2,6,128,128]{3,2,1,0:T(8,128)(2,1)S(1)} collective-permute-done((bf16[2,6,128,128]{3,2,1,0:T(8,128)(2,1)}, bf16[2,6,128,128]{3,2,1,0:T(8,128)(2,1)S(1)}, u32[]{:S(2)}, u32[]{:S(2)}) %collective-permute-start.2) | collective-permute-done | bytes 393248 | tf_op jit(solution)/shard_map/ppermute | solution.py:145
  56.4 4.2 %collective-permute-done.6.refs_2_ = bf16[2,6,128,128]{3,2,1,0:T(8,128)(2,1)S(1)} collective-permute-done((bf16[2,6,128,128]{3,2,1,0:T(8,128)(2,1)S(1)}, bf16[2,6,128,128]{3,2,1,0:T(8,128)(2,1)S(1)}, u32[]{:S(2)}, u32[]{:S(2)}) %collective-permute-start.6) | collective-permute-done | bytes 393248 | tf_op jit(solution)/shard_map/ppermute | solution.py:145
  60.6 1.0 collective-permute-start.7
  61.7 4.2 %collective-permute-done.3.refs_1_ = bf16[2,6,128,128]{3,2,1,0:T(8,128)(2,1)S(1)} collective-permute-done((bf16[2,6,128,128]{3,2,1,0:T(8,128)(2,1)S(1)}, bf16[2,6,128,128]{3,2,1,0:T(8,128)(2,1)S(1)}, u32[]{:S(2)}, u32[]{:S(2)}) %collective-permute-start.3) | collective-permute-done | bytes 393248 | tf_op jit(solution)/shard_map/ppermute | solution.py:145
  65.9 0.7 slice_bitcast_fusion.1
  66.6 4.9 %collective-permute-done.7.refs_2_ = bf16[2,6,128,128]{3,2,1,0:T(8,128)(2,1)S(1)} collective-permute-done((bf16[2,6,128,128]{3,2,1,0:T(8,128)(2,1)S(1)}, bf16[2,6,128,128]{3,2,1,0:T(8,128)(2,1)S(1)}, u32[]{:S(2)}, u32[]{:S(2)}) %collective-permute-start.7) | collective-permute-done | bytes 393248 | tf_op jit(solution)/shard_map/ppermute | solution.py:145
  71.6 0.7 slice_bitcast_fusion
  72.3 1.0 collective-permute-start.8
  73.3 1.1 copy-done.1
  74.5 13.1 %attend768.3.refs_3_ = f32[16,3,128,128]{3,2,1,0:T(8,128)} custom-call(bf16[16,3,128,128]{3,2,1,0:T(8,128)(2,1)} %copy-done.1, bf16[2,6,128,128]{3,2,1,0:T(8,128)(2,1)} %copy-done.4, bf16[2,6,128,128]{3,2,1,0:T(8,128)(2,1)} %collective-permute-done.1.refs_2_, bf16[2,6,128,128]{3,2,1,0:T(8,128)(2,1)} %copy-done.8), custom_call_target="tpu_custom_call" | custom-call | flops 2415919104 | bytes 8388608 | tf_op jit(solution)/shard_map/attend768/pallas_call | solution.py:94
  87.6 12.8 %attend512.6.refs_3_ = f32[16,3,128,128]{3,2,1,0:T(8,128)} custom-call(bf16[16,3,128,128]{3,2,1,0:T(8,128)(2,1)} %copy-done.1, bf16[2,6,128,128]{3,2,1,0:T(8,128)(2,1)} %copy-done.9, bf16[2,6,128,128]{3,2,1,0:T(8,128)(2,1)} %copy-done.10, f32[16,3,128,128]{3,2,1,0:T(8,128)} %attend768.3.refs_3_), custom_call_target="tpu_custom_call", output_to_operand_aliasing={{}: (3, {})} | custom-call | flops 1610612736 | bytes 8388608 | tf_op jit(solution)/shard_map/attend512/pallas_call | solution.py:94
  100.4 12.8 %attend512.7.refs_3_ = f32[16,3,128,128]{3,2,1,0:T(8,128)} custom-call(bf16[16,3,128,128]{3,2,1,0:T(8,128)(2,1)} %copy-done.1, bf16[2,6,128,128]{3,2,1,0:T(8,128)(2,1)} %copy-done.6, bf16[2,6,128,128]{3,2,1,0:T(8,128)(2,1)} %copy-done.7, f32[16,3,128,128]{3,2,1,0:T(8,128)} %attend512.6.refs_3_), custom_call_target="tpu_custom_call", output_to_operand_aliasing={{}: (3, {})} | custom-call | flops 1610612736 | bytes 8388608 | tf_op jit(solution)/shard_map/attend512/pallas_call | solution.py:94
  113.2 0.7 copy-done.2
  113.9 0.7 copy-done.3
  114.6 10.8 %attend256.3 = bf16[16,3,128,128]{3,2,1,0:T(8,128)(2,1)} custom-call(bf16[16,3,128,128]{3,2,1,0:T(8,128)(2,1)} %copy-done.1, bf16[6,128,128]{2,1,0:T(8,128)(2,1)} %copy-done.2, bf16[6,128,128]{2,1,0:T(8,128)(2,1)} %copy-done.3, f32[16,3,128,128]{3,2,1,0:T(8,128)} %attend512.7.refs_3_), custom_call_target="tpu_custom_call" | custom-call | flops 805306368 | bytes 8388608 | tf_op jit(solution)/shard_map/attend256/pallas_call | solution.py:94
  125.4 13.2 %attend768.2.refs_3_ = f32[16,3,128,128]{3,2,1,0:T(8,128)} custom-call(bf16[16,3,128,128]{3,2,1,0:T(8,128)(2,1)} %copy-done, bf16[2,6,128,128]{3,2,1,0:T(8,128)(2,1)} %copy-done.4, bf16[2,6,128,128]{3,2,1,0:T(8,128)(2,1)} %collective-permute-done.1.refs_2_, bf16[2,6,128,128]{3,2,1,0:T(8,128)(2,1)} %copy-done.8), custom_call_target="tpu_custom_call" | custom-call | flops 2415919104 | bytes 8388608 | tf_op jit(solution)/shard_map/attend768/pallas_call | solution.py:94
  138.6 12.8 %attend512.4.refs_3_ = f32[16,3,128,128]{3,2,1,0:T(8,128)} custom-call(bf16[16,3,128,128]{3,2,1,0:T(8,128)(2,1)} %copy-done, bf16[2,6,128,128]{3,2,1,0:T(8,128)(2,1)} %copy-done.9, bf16[2,6,128,128]{3,2,1,0:T(8,128)(2,1)} %copy-done.10, f32[16,3,128,128]{3,2,1,0:T(8,128)} %attend768.2.refs_3_), custom_call_target="tpu_custom_call", output_to_operand_aliasing={{}: (3, {})} | custom-call | flops 1610612736 | bytes 8388608 | tf_op jit(solution)/shard_map/attend512/pallas_call | solution.py:94
  151.4 12.8 %attend512.5.refs_3_ = f32[16,3,128,128]{3,2,1,0:T(8,128)} custom-call(bf16[16,3,128,128]{3,2,1,0:T(8,128)(2,1)} %copy-done, bf16[2,6,128,128]{3,2,1,0:T(8,128)(2,1)} %copy-done.6, bf16[2,6,128,128]{3,2,1,0:T(8,128)(2,1)} %copy-done.7, f32[16,3,128,128]{3,2,1,0:T(8,128)} %attend512.4.refs_3_), custom_call_target="tpu_custom_call", output_to_operand_aliasing={{}: (3, {})} | custom-call | flops 1610612736 | bytes 8388608 | tf_op jit(solution)/shard_map/attend512/pallas_call | solution.py:94
  164.2 10.8 %attend256.2 = bf16[16,3,128,128]{3,2,1,0:T(8,128)(2,1)} custom-call(bf16[16,3,128,128]{3,2,1,0:T(8,128)(2,1)} %copy-done, bf16[6,128,128]{2,1,0:T(8,128)(2,1)} %copy-done.2, bf16[6,128,128]{2,1,0:T(8,128)(2,1)} %copy-done.3, f32[16,3,128,128]{3,2,1,0:T(8,128)} %attend512.5.refs_3_), custom_call_target="tpu_custom_call" | custom-call | flops 805306368 | bytes 8388608 | tf_op jit(solution)/shard_map/attend256/pallas_call | solution.py:94
  174.9 2.0 add_convert_fusion
  176.9 28.0 %all_to_all.10.parts_ref = bf16[16,3,128,128]{3,2,1,0:T(8,128)(2,1)} all-to-all(bf16[16,3,128,128]{3,2,1,0:T(8,128)(2,1)S(1)} %add_convert_fusion), channel_id=1, replica_groups=mesh['xh'=2,'z'=8,'xl'=2,'y'=4,'c'=2] {'xh','xl','y'}, dimensions={0} | all-to-all | bytes 3145728 | tf_op jit(solution)/shard_map/all_to_all | solution.py:159
  204.9 2.4 %finish.1 = bf16[128,768]{1,0:T(8,128)(2,1)} custom-call(bf16[16,3,128,128]{3,2,1,0:T(8,128)(2,1)} %all_to_all.10.parts_ref), custom_call_target="tpu_custom_call" | custom-call | tf_op jit(solution)/shard_map/finish/pallas_call | solution.py:117
  (31 shorter events, 0.1 us)
Async XLA Ops:
  2.9 7.2 %copy-start.11 = (bf16[6,128,128]{2,1,0:T(8,128)(2,1)S(1)}, bf16[6,128,128]{2,1,0:T(8,128)(2,1)}, u32[]{:S(2)}) copy-start(bf16[6,128,128]{2,1,0:T(8,128)(2,1)} %get-tuple-element.10) | copy-start | bytes 589828
  2.9 31.7 %copy-start.5 = (bf16[6,128,128]{2,1,0:T(8,128)(2,1)S(1)}, bf16[6,128,128]{2,1,0:T(8,128)(2,1)}, u32[]{:S(2)}) copy-start(bf16[6,128,128]{2,1,0:T(8,128)(2,1)} %get-tuple-element.9) | copy-start | bytes 589828
  2.9 33.8 %all-to-all-start = ((bf16[16,3,128,128]{3,2,1,0:T(8,128)(2,1)}), bf16[16,3,128,128]{3,2,1,0:T(8,128)(2,1)S(1)}, u32[]{:S(2)}, u32[]{:S(2)}) async-start(bf16[16,3,128,128]{3,2,1,0:T(8,128)(2,1)} %get-tuple-element.8), calls=%async_computation | async-start | bytes 3145728 | tf_op jit(solution)/shard_map/all_to_all | solution.py:140
  10.1 24.5 %collective-permute-start = (bf16[6,128,128]{2,1,0:T(8,128)(2,1)S(1)}, bf16[6,128,128]{2,1,0:T(8,128)(2,1)S(1)}, u32[]{:S(2)}, u32[]{:S(2)}) collective-permute-start(bf16[6,128,128]{2,1,0:T(8,128)(2,1)S(1)} %copy-done.11), channel_id=1, source_target_pairs={{0,136},{136,0},{8,128},{128,8},{1,137},{137,1},{9,129},{129,9},{2... | collective-permute-start | bytes 589832 | tf_op jit(solution)/shard_map/ppermute | solution.py:139
  34.6 31.3 %copy-start.4 = (bf16[2,6,128,128]{3,2,1,0:T(8,128)(2,1)}, bf16[2,6,128,128]{3,2,1,0:T(8,128)(2,1)S(1)}, u32[]{:S(2)}) copy-start(bf16[2,6,128,128]{3,2,1,0:T(8,128)(2,1)S(1)} %pad_maximum_fusion.refs_1_) | copy-start | bytes 1179652
  34.6 9.9 %collective-permute-start.1 = (bf16[2,6,128,128]{3,2,1,0:T(8,128)(2,1)S(1)}, bf16[2,6,128,128]{3,2,1,0:T(8,128)(2,1)}, u32[]{:S(2)}, u32[]{:S(2)}) collective-permute-start(bf16[2,6,128,128]{3,2,1,0:T(8,128)(2,1)S(1)} %pad_maximum_fusion.refs_1_), channel_id=1, source_target_pairs={{0,16},{16,32},{32,48},{48,64},{64,80},{80,96},{96,112},{112,0},{1... | collective-permute-start | bytes 1179656 | tf_op jit(solution)/shard_map/ppermute | solution.py:145
  36.6 51.0 %copy-start = (bf16[16,3,128,128]{3,2,1,0:T(8,128)(2,1)}, bf16[16,3,128,128]{3,2,1,0:T(8,128)(2,1)S(1)}, u32[]{:S(2)}) copy-start(bf16[16,3,128,128]{3,2,1,0:T(8,128)(2,1)S(1)} %all-to-all-done.refs_0_) | copy-start | bytes 4718596
  36.6 36.7 %collective-permute-start.9 = (bf16[16,3,128,128]{3,2,1,0:T(8,128)(2,1)S(1)}, bf16[16,3,128,128]{3,2,1,0:T(8,128)(2,1)S(1)}, u32[]{:S(2)}, u32[]{:S(2)}) collective-permute-start(bf16[16,3,128,128]{3,2,1,0:T(8,128)(2,1)S(1)} %all-to-all-done.refs_0_), channel_id=1, source_target_pairs={{0,1},{1,0},{2,3},{3,2},{4,5},{5,4},{6,7},{7,6},{8,9},{9,8},{10,11... | collective-permute-start | bytes 4718600 | tf_op jit(solution)/shard_map/ppermute | solution.py:149
  36.6 11.7 %collective-permute-start.5 = (bf16[2,6,128,128]{3,2,1,0:T(8,128)(2,1)S(1)}, bf16[2,6,128,128]{3,2,1,0:T(8,128)(2,1)S(1)}, u32[]{:S(2)}, u32[]{:S(2)}) collective-permute-start(bf16[2,6,128,128]{3,2,1,0:T(8,128)(2,1)S(1)} %pad_maximum_fusion.refs_1_), channel_id=1, source_target_pairs={{0,112},{16,0},{32,16},{48,32},{64,48},{80,64},{96,80},{112,96},{1... | collective-permute-start | bytes 1179656 | tf_op jit(solution)/shard_map/ppermute | solution.py:145
  44.5 11.8 %collective-permute-start.2 = (bf16[2,6,128,128]{3,2,1,0:T(8,128)(2,1)}, bf16[2,6,128,128]{3,2,1,0:T(8,128)(2,1)S(1)}, u32[]{:S(2)}, u32[]{:S(2)}) collective-permute-start(bf16[2,6,128,128]{3,2,1,0:T(8,128)(2,1)} %collective-permute-done.1.refs_2_), channel_id=1, source_target_pairs={{0,16},{16,32},{32,48},{48,64},{64,80},{80,96},{96,112},{112,0},{1... | collective-permute-start | bytes 1179656 | tf_op jit(solution)/shard_map/ppermute | solution.py:145
  48.3 12.3 %copy-start.8 = (bf16[2,6,128,128]{3,2,1,0:T(8,128)(2,1)}, bf16[2,6,128,128]{3,2,1,0:T(8,128)(2,1)S(1)}, u32[]{:S(2)}) copy-start(bf16[2,6,128,128]{3,2,1,0:T(8,128)(2,1)S(1)} %collective-permute-done.5.refs_3_) | copy-start | bytes 1179652
  48.3 12.3 %collective-permute-start.6 = (bf16[2,6,128,128]{3,2,1,0:T(8,128)(2,1)S(1)}, bf16[2,6,128,128]{3,2,1,0:T(8,128)(2,1)S(1)}, u32[]{:S(2)}, u32[]{:S(2)}) collective-permute-start(bf16[2,6,128,128]{3,2,1,0:T(8,128)(2,1)S(1)} %collective-permute-done.5.refs_3_), channel_id=1, source_target_pairs={{0,112},{16,0},{32,16},{48,32},{64,48},{80,64},{96,80},{112,96},{1... | collective-permute-start | bytes 1179656 | tf_op jit(solution)/shard_map/ppermute | solution.py:145
  56.4 5.3 %copy-start.9 = (bf16[2,6,128,128]{3,2,1,0:T(8,128)(2,1)}, bf16[2,6,128,128]{3,2,1,0:T(8,128)(2,1)S(1)}, u32[]{:S(2)}) copy-start(bf16[2,6,128,128]{3,2,1,0:T(8,128)(2,1)S(1)} %collective-permute-done.2.refs_1_) | copy-start | bytes 1179652
  56.4 9.5 %collective-permute-start.3 = (bf16[2,6,128,128]{3,2,1,0:T(8,128)(2,1)S(1)}, bf16[2,6,128,128]{3,2,1,0:T(8,128)(2,1)S(1)}, u32[]{:S(2)}, u32[]{:S(2)}) collective-permute-start(bf16[2,6,128,128]{3,2,1,0:T(8,128)(2,1)S(1)} %collective-permute-done.2.refs_1_), channel_id=1, source_target_pairs={{0,16},{16,32},{32,48},{48,64},{64,80},{80,96},{96,112},{112,0},{1... | collective-permute-start | bytes 1179656 | tf_op jit(solution)/shard_map/ppermute | solution.py:145
  60.6 12.7 %copy-start.10 = (bf16[2,6,128,128]{3,2,1,0:T(8,128)(2,1)}, bf16[2,6,128,128]{3,2,1,0:T(8,128)(2,1)S(1)}, u32[]{:S(2)}) copy-start(bf16[2,6,128,128]{3,2,1,0:T(8,128)(2,1)S(1)} %collective-permute-done.6.refs_2_) | copy-start | bytes 1179652
  60.6 11.0 %collective-permute-start.7 = (bf16[2,6,128,128]{3,2,1,0:T(8,128)(2,1)S(1)}, bf16[2,6,128,128]{3,2,1,0:T(8,128)(2,1)S(1)}, u32[]{:S(2)}, u32[]{:S(2)}) collective-permute-start(bf16[2,6,128,128]{3,2,1,0:T(8,128)(2,1)S(1)} %collective-permute-done.6.refs_2_), channel_id=1, source_target_pairs={{0,112},{16,0},{32,16},{48,32},{64,48},{80,64},{96,80},{112,96},{1... | collective-permute-start | bytes 1179656 | tf_op jit(solution)/shard_map/ppermute | solution.py:145
  65.9 6.4 %copy-start.6 = (bf16[2,6,128,128]{3,2,1,0:T(8,128)(2,1)}, bf16[2,6,128,128]{3,2,1,0:T(8,128)(2,1)S(1)}, u32[]{:S(2)}) copy-start(bf16[2,6,128,128]{3,2,1,0:T(8,128)(2,1)S(1)} %collective-permute-done.3.refs_1_) | copy-start | bytes 1179652
  66.6 46.6 %collective-permute-start.4 = (bf16[6,128,128]{2,1,0:T(8,128)(2,1)}, bf16[6,128,128]{2,1,0:T(8,128)(2,1)S(1)}, u32[]{:S(2)}, u32[]{:S(2)}) collective-permute-start(bf16[6,128,128]{2,1,0:T(8,128)(2,1)} %slice_bitcast_fusion.1), channel_id=1, source_target_pairs={{0,16},{16,32},{32,48},{48,64},{64,80},{80,96},{96,112},{112,0},{1... | collective-permute-start | bytes 589832 | tf_op jit(solution)/shard_map/ppermute | solution.py:147
  71.6 1.8 copy-start.7
  72.3 40.9 %collective-permute-start.8 = (bf16[6,128,128]{2,1,0:T(8,128)(2,1)}, bf16[6,128,128]{2,1,0:T(8,128)(2,1)S(1)}, u32[]{:S(2)}, u32[]{:S(2)}) collective-permute-start(bf16[6,128,128]{2,1,0:T(8,128)(2,1)} %slice_bitcast_fusion), channel_id=1, source_target_pairs={{0,112},{16,0},{32,16},{48,32},{64,48},{80,64},{96,80},{112,96},{1... | collective-permute-start | bytes 589832 | tf_op jit(solution)/shard_map/ppermute | solution.py:147
  73.3 1.2 copy-start.1
  113.2 0.7 copy-start.2
  113.9 0.7 copy-start.3
  125.4 49.6 %collective-permute-start.10 = (bf16[16,3,128,128]{3,2,1,0:T(8,128)(2,1)}, bf16[16,3,128,128]{3,2,1,0:T(8,128)(2,1)S(1)}, u32[]{:S(2)}, u32[]{:S(2)}) collective-permute-start(bf16[16,3,128,128]{3,2,1,0:T(8,128)(2,1)} %attend256.3), channel_id=1, source_target_pairs={{0,1},{1,0},{2,3},{3,2},{4,5},{5,4},{6,7},{7,6},{8,9},{9,8},{10,11... | collective-permute-start | bytes 4718600 | tf_op jit(solution)/shard_map/ppermute | solution.py:157

commit v2 on v1

v2 whole, which is shorter than its diff:
```python
import functools
import math

import jax
import jax.numpy as jnp
from jax import lax
from jax.experimental import pallas as pl
from jax.experimental.pallas import tpu as pltpu
from jax.sharding import Mesh
from jax.sharding import PartitionSpec as P

AXES = ("xh", "z", "xl", "y", "c")
PLANE = ("xh", "xl", "y")
HEADS = 6
DH = 128
HALF = 3
EPSILON = 0.1
SLOPE = -math.log2(math.e) / math.sqrt(DH)

VM = pl.BlockSpec(memory_space=pltpu.VMEM)
AHEAD = 2
LAG = 2
SM = pl.BlockSpec(memory_space=pltpu.SMEM)


def normed(ref, gain_ref, h):
    x = ref[:, h * DH : (h + 1) * DH].astype(jnp.float32)
    inverse = lax.rsqrt(jnp.mean(x * x, axis=-1, keepdims=True) + EPSILON)
    return x * inverse * gain_ref[...]


def keys_body(half_ref, k_ref, v_ref, kg_ref, mine_ref, other_ref, both):
    half = half_ref[0]
    for h in range(HEADS):
        g, i = h // HALF, h % HALF
        both[g, i] = normed(k_ref, kg_ref, h).astype(jnp.bfloat16)
        v = v_ref[:, h * DH : (h + 1) * DH].astype(jnp.float32)
        both[g, HALF + i] = v.T.astype(jnp.bfloat16)
    mine_ref[...] = both[half]
    other_ref[...] = both[1 - half]


def queries_body(q_ref, qg_ref, after_ref, qt_ref):
    for h in range(HEADS):
        g, i = h // HALF, h % HALF
        qt = normed(q_ref, qg_ref, h).T.astype(jnp.bfloat16)
        for d in range(8):
            qt_ref[g * 8 + d, i] = qt


def prepare_keys(half, k, v, kg):
    rows = k.shape[0]
    pack = jax.ShapeDtypeStruct((2 * HALF, DH, rows), jnp.bfloat16)
    return pl.pallas_call(
        keys_body,
        out_shape=(pack, pack),
        in_specs=[SM] + [VM] * 3,
        out_specs=(VM, VM),
        scratch_shapes=[pltpu.VMEM((2, 2 * HALF, DH, rows), jnp.bfloat16)],
        compiler_params=pltpu.CompilerParams(vmem_limit_bytes=60 << 20),
        name="prepare_keys",
    )(half, k, v, kg)


def prepare_queries(q, qg, after):
    rows = q.shape[0]
    return pl.pallas_call(
        queries_body,
        out_shape=jax.ShapeDtypeStruct((16, HALF, DH, rows), jnp.bfloat16),
        in_specs=[VM, VM, pl.BlockSpec(memory_space=pl.ANY)],
        out_specs=VM,
        compiler_params=pltpu.CompilerParams(vmem_limit_bytes=60 << 20),
        name="prepare_queries",
    )(q, qg, after)


def attend_body(tokens, n, tiles, first, last, *refs):
    qt, out = refs[0], refs[-1]
    units = refs[1 : 1 + n]
    total_in = None if first else refs[1 + n]
    shift = 1.0 / tokens

    pairs = tuple(zip(units[::2], units[1::2]))
    unroll = max(1, tiles // (len(pairs) * HALF))

    def scores(i, h, p):
        a, b = pairs[p]
        q = jnp.concatenate([qt[2 * i, h], qt[2 * i + 1, h]], axis=1)
        k = jnp.concatenate([a[h], b[h]], axis=0)
        return jnp.dot(k, q, preferred_element_type=jnp.float32)

    def weigh(s):
        u = jnp.exp2(s * SLOPE) + shift
        return jnp.bfloat16(1.0) / u.astype(jnp.bfloat16)

    def mixed(h, p, w):
        a, b = pairs[p]
        vt = jnp.concatenate([a[HALF + h], b[HALF + h]], axis=1)
        return jnp.dot(vt, w, preferred_element_type=jnp.float32)

    def store(i, h, total):
        for j in range(2):
            r = total[:, DH * j : DH * (j + 1)]
            if not first:
                r = r + total_in[2 * i + j, h]
            out[2 * i + j, h] = (r * shift).astype(jnp.bfloat16) if last else r

    def group(g, _):
        steps = [
            (g * unroll + t, h, p)
            for t in range(unroll)
            for h in range(HALF)
            for p in range(len(pairs))
        ]
        count = len(steps)
        ahead = [scores(*steps[t]) for t in range(min(AHEAD, count))]
        weights = []
        total = None
        for t in range(count + LAG):
            if t + AHEAD < count:
                ahead.append(scores(*steps[t + AHEAD]))
            if t < count:
                weights.append(weigh(ahead.pop(0)))
            if t >= LAG:
                i, h, p = steps[t - LAG]
                o = mixed(h, p, weights.pop(0))
                total = o if p == 0 else total + o
                if p == len(pairs) - 1:
                    store(i, h, total)
        return 0

    lax.fori_loop(0, 8 // unroll, group, 0)


def attend(tokens, qt, blocks, total, last, tiles=24):
    first = total is None
    args = [qt, *blocks] + ([] if first else [total])
    keys = 128 * len(blocks)
    pairs = keys * 2048 * HALF
    return pl.pallas_call(
        functools.partial(attend_body, tokens, len(blocks), tiles, first, last),
        out_shape=jax.ShapeDtypeStruct(qt.shape, jnp.bfloat16 if last else jnp.float32),
        in_specs=[VM] * len(args),
        out_specs=VM,
        input_output_aliases={} if first or last else {len(args) - 1: 0},
        cost_estimate=pl.CostEstimate(
            flops=pairs * DH * 4, bytes_accessed=8 << 20, transcendentals=2 * pairs
        ),
        compiler_params=pltpu.CompilerParams(vmem_limit_bytes=16 << 20),
    )(*args)


def finish_body(parts_ref, out_ref):
    for h in range(HEADS):
        g, i = h // HALF, h % HALF
        total = parts_ref[g * 8, i].astype(jnp.float32)
        for s in range(1, 8):
            total = total + parts_ref[g * 8 + s, i].astype(jnp.float32)
        out_ref[:, h * DH : (h + 1) * DH] = total.T.astype(jnp.bfloat16)


def finish(parts, rows):
    return pl.pallas_call(
        finish_body,
        out_shape=jax.ShapeDtypeStruct((rows, HEADS * DH), jnp.bfloat16),
        in_specs=[VM],
        out_specs=VM,
        compiler_params=pltpu.CompilerParams(vmem_limit_bytes=8 << 20),
        name="finish",
    )(parts)


def per_device(queries, keys, values, query_gain, key_gain):
    rows = queries.shape[0]
    tokens = rows * lax.axis_size(AXES)
    half = lax.axis_index("xh").astype(jnp.int32).reshape(1)
    mine, other = prepare_keys(half, keys, values, key_gain.reshape(1, DH))
    qt_send = prepare_queries(queries, query_gain.reshape(1, DH), other)
    partner = [(0, 3), (3, 0), (1, 2), (2, 1)]
    n = lax.axis_size("z")
    ring = [(2 * i, 2 * ((i + 1) % n)) for i in range(n)]
    ring += [(2 * i + 1, 2 * ((i - 1) % n) + 1) for i in range(n)]
    swap = [(0, 1), (1, 0)]

    a, b = [mine], []
    b.append(lax.ppermute(other, ("xh", "xl"), partner))
    own = lax.all_to_all(qt_send, PLANE, 0, 0, tiled=True)
    for _ in range(1, n):
        a.append(lax.ppermute(a[-1], ("z", "c"), ring))
        b.append(lax.ppermute(b[-1], ("z", "c"), ring))
    peer = lax.ppermute(own, "c", swap)

    groups = [a[0:4] + b[0:4], a[4:6] + b[4:6], a[6:8] + b[6:8]]
    totals = [None, None]
    for s, group in enumerate(groups):
        last = s == len(groups) - 1
        for who in (1, 0) if last else (0, 1):
            totals[who] = attend(tokens, (own, peer)[who], group, totals[who], last)
    back = lax.ppermute(totals[1], "c", swap)
    parts = (totals[0].astype(jnp.float32) + back.astype(jnp.float32)).astype(jnp.bfloat16)
    parts = lax.all_to_all(parts, PLANE, 0, 0, tiled=True)
    return finish(parts, rows)


def solution(mesh):
    torus = Mesh(mesh.devices.reshape(2, 8, 2, 4, 2), AXES)

    return jax.shard_map(
        per_device,
        mesh=torus,
        in_specs=(P(AXES, None), P(AXES, None), P(AXES, None), P(), P()),
        out_specs=P(AXES, None),
        check_vma=False,
    )
```

time: 210 us -> 148 us (0.70)
  the two profiles are of different devices: /device:TPU:32 before, /device:TPU:96 now
where the time goes in v2:
time: 148 us; the launch traced here: 147 us
  blocking collectives  56.2 us (38%)
  starting transfers between devices  41.5 us (28%)
  Pallas kernels  37.2 us (25%)
  waiting for transfers between devices  11.5 us (8%)
    pallas_call x6, Pallas kernels, attend(): pl.pallas_call(functools.partial(attend_body, tokens, len(blocks), tiles,...  31.7 us
    all_to_all x1, blocking collectives, per_device(): own = lax.all_to_all(qt_send, PLANE, 0, 0, tiled=True)  29.7 us
    all_to_all x1, blocking collectives, per_device(): parts = lax.all_to_all(parts, PLANE, 0, 0, tiled=True)  26.5 us
    ppermute x7, starting transfers between devices, per_device(): b.append(lax.ppermute(b[-1], ('z', 'c'), ring))  25.3 us
    ppermute x7, starting transfers between devices, per_device(): a.append(lax.ppermute(a[-1], ('z', 'c'), ring))  14.7 us
    ppermute x7, waiting for transfers between devices, per_device(): b.append(lax.ppermute(b[-1], ('z', 'c'), ring))  7.58 us
    ppermute x1, waiting for transfers between devices, per_device(): b.append(lax.ppermute(other, ('xh', 'xl'), partner))  3.93 us
  transfers between devices with their start and end apart: 17, of which 7 were waited for; matrix products, arithmetic and copies ran while one was open for 0% of the time, Pallas kernels for 19%

profile of v2, /device:TPU:96, one launch (start us, length us, event | category | flops | bytes accessed | tf_op | source)
XLA Modules:
  0.0 147.3 jit_solution(17351942488937613608)
XLA Ops:
  0.0 2.0 %prepare_keys.1 = (bf16[6,128,128]{2,1,0:T(8,128)(2,1)}, bf16[6,128,128]{2,1,0:T(8,128)(2,1)}) custom-call(s32[1]{0:T(128)} %bitcast.1.half_ref, bf16[128,768]{1,0:T(8,128)(2,1)} %k_ref.1, bf16[128,768]{1,0:T(8,128)(2,1)} %v_ref.1, f32[1,128]{1,0:T(1,128)} %bitcast.3), custom_call_target="tpu_custom_call" | custom-call | tf_op jit(solution)/shard_map/prepare_keys/pallas_call | solution.py:54
  2.0 2.5 %prepare_queries.1 = bf16[16,3,128,128]{3,2,1,0:T(8,128)(2,1)} custom-call(bf16[128,768]{1,0:T(8,128)(2,1)} %q_ref.1, f32[1,128]{1,0:T(1,128)} %bitcast.4, bf16[6,128,128]{2,1,0:T(8,128)(2,1)} %get-tuple-element.7.after_ref), custom_call_target="tpu_custom_call" | custom-call | tf_op jit(solution)/shard_map/prepare_queries/pallas_call | solution.py:67
  4.6 29.7 %all_to_all.10.refs_0_ = bf16[16,3,128,128]{3,2,1,0:T(8,128)(2,1)S(1)} all-to-all(bf16[16,3,128,128]{3,2,1,0:T(8,128)(2,1)} %prepare_queries.1), channel_id=1, replica_groups=mesh['xh'=2,'z'=8,'xl'=2,'y'=4,'c'=2] {'xh','xl','y'}, dimensions={0} | all-to-all | bytes 3145728 | tf_op jit(solution)/shard_map/all_to_all | solution.py:187
  34.3 1.5 collective-permute-start.7
  35.7 3.1 %collective-permute-start = (bf16[6,128,128]{2,1,0:T(8,128)(2,1)S(1)}, bf16[6,128,128]{2,1,0:T(8,128)(2,1)S(1)}, u32[]{:S(2)}, u32[]{:S(2)}) collective-permute-start(bf16[6,128,128]{2,1,0:T(8,128)(2,1)S(1)} %copy-done), channel_id=1, source_target_pairs={{0,16},{16,32},{32,48},{48,64},{64,80},{80,96},{96,112},{112,0},{1... | collective-permute-start | bytes 589832 | tf_op jit(solution)/shard_map/ppermute | solution.py:189
  38.9 3.9 %collective-permute-done.7.refs_5_ = bf16[6,128,128]{2,1,0:T(8,128)(2,1)S(1)} collective-permute-done((bf16[6,128,128]{2,1,0:T(8,128)(2,1)S(1)}, bf16[6,128,128]{2,1,0:T(8,128)(2,1)S(1)}, u32[]{:S(2)}, u32[]{:S(2)}) %collective-permute-start.7) | collective-permute-done | bytes 196640 | tf_op jit(solution)/shard_map/ppermute | solution.py:186
  42.8 3.1 %collective-permute-start.8 = (bf16[6,128,128]{2,1,0:T(8,128)(2,1)S(1)}, bf16[6,128,128]{2,1,0:T(8,128)(2,1)S(1)}, u32[]{:S(2)}, u32[]{:S(2)}) collective-permute-start(bf16[6,128,128]{2,1,0:T(8,128)(2,1)S(1)} %collective-permute-done.7.refs_5_), channel_id=1, source_target_pairs={{0,16},{16,32},{32,48},{48,64},{64,80},{80,96},{96,112},{112,0},{1... | collective-permute-start | bytes 589832 | tf_op jit(solution)/shard_map/ppermute | solution.py:190
  45.9 1.0 collective-permute-start.1
  47.0 2.2 %collective-permute-done.8.refs_6_ = bf16[6,128,128]{2,1,0:T(8,128)(2,1)S(1)} collective-permute-done((bf16[6,128,128]{2,1,0:T(8,128)(2,1)S(1)}, bf16[6,128,128]{2,1,0:T(8,128)(2,1)S(1)}, u32[]{:S(2)}, u32[]{:S(2)}) %collective-permute-start.8) | collective-permute-done | bytes 196640 | tf_op jit(solution)/shard_map/ppermute | solution.py:190
  49.1 3.7 %collective-permute-start.9 = (bf16[6,128,128]{2,1,0:T(8,128)(2,1)S(1)}, bf16[6,128,128]{2,1,0:T(8,128)(2,1)S(1)}, u32[]{:S(2)}, u32[]{:S(2)}) collective-permute-start(bf16[6,128,128]{2,1,0:T(8,128)(2,1)S(1)} %collective-permute-done.8.refs_6_), channel_id=1, source_target_pairs={{0,16},{16,32},{32,48},{48,64},{64,80},{80,96},{96,112},{112,0},{1... | collective-permute-start | bytes 589832 | tf_op jit(solution)/shard_map/ppermute | solution.py:190
  52.8 2.1 %collective-permute-start.2 = (bf16[6,128,128]{2,1,0:T(8,128)(2,1)S(1)}, bf16[6,128,128]{2,1,0:T(8,128)(2,1)S(1)}, u32[]{:S(2)}, u32[]{:S(2)}) collective-permute-start(bf16[6,128,128]{2,1,0:T(8,128)(2,1)S(1)} %collective-permute-done.1.refs_3_), channel_id=1, source_target_pairs={{0,16},{16,32},{32,48},{48,64},{64,80},{80,96},{96,112},{112,0},{1... | collective-permute-start | bytes 589832 | tf_op jit(solution)/shard_map/ppermute | solution.py:189
  54.9 1.1 collective-permute-done.9.refs_7_
  56.0 3.7 %collective-permute-start.10 = (bf16[6,128,128]{2,1,0:T(8,128)(2,1)S(1)}, bf16[6,128,128]{2,1,0:T(8,128)(2,1)S(1)}, u32[]{:S(2)}, u32[]{:S(2)}) collective-permute-start(bf16[6,128,128]{2,1,0:T(8,128)(2,1)S(1)} %collective-permute-done.9.refs_7_), channel_id=1, source_target_pairs={{0,16},{16,32},{32,48},{48,64},{64,80},{80,96},{96,112},{112,0},{1... | collective-permute-start | bytes 589832 | tf_op jit(solution)/shard_map/ppermute | solution.py:190
  59.7 2.1 %collective-permute-start.3 = (bf16[6,128,128]{2,1,0:T(8,128)(2,1)S(1)}, bf16[6,128,128]{2,1,0:T(8,128)(2,1)S(1)}, u32[]{:S(2)}, u32[]{:S(2)}) collective-permute-start(bf16[6,128,128]{2,1,0:T(8,128)(2,1)S(1)} %collective-permute-done.2.refs_4_), channel_id=1, source_target_pairs={{0,16},{16,32},{32,48},{48,64},{64,80},{80,96},{96,112},{112,0},{1... | collective-permute-start | bytes 589832 | tf_op jit(solution)/shard_map/ppermute | solution.py:189
  61.8 1.1 collective-permute-done.10.refs_8_
  62.9 3.7 %collective-permute-start.11 = (bf16[6,128,128]{2,1,0:T(8,128)(2,1)S(1)}, bf16[6,128,128]{2,1,0:T(8,128)(2,1)S(1)}, u32[]{:S(2)}, u32[]{:S(2)}) collective-permute-start(bf16[6,128,128]{2,1,0:T(8,128)(2,1)S(1)} %collective-permute-done.10.refs_8_), channel_id=1, source_target_pairs={{0,16},{16,32},{32,48},{48,64},{64,80},{80,96},{96,112},{112,0},{1... | collective-permute-start | bytes 589832 | tf_op jit(solution)/shard_map/ppermute | solution.py:190
  66.6 2.1 %collective-permute-start.4 = (bf16[6,128,128]{2,1,0:T(8,128)(2,1)S(1)}, bf16[6,128,128]{2,1,0:T(8,128)(2,1)S(1)}, u32[]{:S(2)}, u32[]{:S(2)}) collective-permute-start(bf16[6,128,128]{2,1,0:T(8,128)(2,1)S(1)} %collective-permute-done.3.refs_1_), channel_id=1, source_target_pairs={{0,16},{16,32},{32,48},{48,64},{64,80},{80,96},{96,112},{112,0},{1... | collective-permute-start | bytes 589832 | tf_op jit(solution)/shard_map/ppermute | solution.py:189
  68.7 1.1 collective-permute-done.11.refs_3_
  69.8 3.7 %collective-permute-start.12 = (bf16[6,128,128]{2,1,0:T(8,128)(2,1)S(1)}, bf16[6,128,128]{2,1,0:T(8,128)(2,1)S(1)}, u32[]{:S(2)}, u32[]{:S(2)}) collective-permute-start(bf16[6,128,128]{2,1,0:T(8,128)(2,1)S(1)} %collective-permute-done.11.refs_3_), channel_id=1, source_target_pairs={{0,16},{16,32},{32,48},{48,64},{64,80},{80,96},{96,112},{112,0},{1... | collective-permute-start | bytes 589832 | tf_op jit(solution)/shard_map/ppermute | solution.py:190
  73.5 2.1 %collective-permute-start.5 = (bf16[6,128,128]{2,1,0:T(8,128)(2,1)S(1)}, bf16[6,128,128]{2,1,0:T(8,128)(2,1)S(1)}, u32[]{:S(2)}, u32[]{:S(2)}) collective-permute-start(bf16[6,128,128]{2,1,0:T(8,128)(2,1)S(1)} %collective-permute-done.4.refs_2_), channel_id=1, source_target_pairs={{0,16},{16,32},{32,48},{48,64},{64,80},{80,96},{96,112},{112,0},{1... | collective-permute-start | bytes 589832 | tf_op jit(solution)/shard_map/ppermute | solution.py:189
  75.6 1.1 collective-permute-done.12.refs_4_
  76.6 3.7 %collective-permute-start.13 = (bf16[6,128,128]{2,1,0:T(8,128)(2,1)S(1)}, bf16[6,128,128]{2,1,0:T(8,128)(2,1)S(1)}, u32[]{:S(2)}, u32[]{:S(2)}) collective-permute-start(bf16[6,128,128]{2,1,0:T(8,128)(2,1)S(1)} %collective-permute-done.12.refs_4_), channel_id=1, source_target_pairs={{0,16},{16,32},{32,48},{48,64},{64,80},{80,96},{96,112},{112,0},{1... | collective-permute-start | bytes 589832 | tf_op jit(solution)/shard_map/ppermute | solution.py:190
  80.3 2.1 %collective-permute-start.6 = (bf16[6,128,128]{2,1,0:T(8,128)(2,1)S(1)}, bf16[6,128,128]{2,1,0:T(8,128)(2,1)S(1)}, u32[]{:S(2)}, u32[]{:S(2)}) collective-permute-start(bf16[6,128,128]{2,1,0:T(8,128)(2,1)S(1)} %collective-permute-done.5.refs_1_), channel_id=1, source_target_pairs={{0,16},{16,32},{32,48},{48,64},{64,80},{80,96},{96,112},{112,0},{1... | collective-permute-start | bytes 589832 | tf_op jit(solution)/shard_map/ppermute | solution.py:189
  82.4 1.1 collective-permute-done.13.refs_3_
  83.5 3.7 %collective-permute-start.14 = (bf16[6,128,128]{2,1,0:T(8,128)(2,1)S(1)}, bf16[6,128,128]{2,1,0:T(8,128)(2,1)S(1)}, u32[]{:S(2)}, u32[]{:S(2)}) collective-permute-start(bf16[6,128,128]{2,1,0:T(8,128)(2,1)S(1)} %collective-permute-done.13.refs_3_), channel_id=1, source_target_pairs={{0,16},{16,32},{32,48},{48,64},{64,80},{80,96},{96,112},{112,0},{1... | collective-permute-start | bytes 589832 | tf_op jit(solution)/shard_map/ppermute | solution.py:190
  87.2 7.9 %shard_map.58.refs_5_ = f32[16,3,128,128]{3,2,1,0:T(8,128)S(1)} custom-call(bf16[16,3,128,128]{3,2,1,0:T(8,128)(2,1)S(1)} %collective-permute-done.15.refs_0_, bf16[6,128,128]{2,1,0:T(8,128)(2,1)S(1)} %copy-done, bf16[6,128,128]{2,1,0:T(8,128)(2,1)S(1)} %collective-permute-done.refs_2_, bf16[6,128,128]{2,1,0:T(8,128)(2,1)S(1)} %collective-permute-done.1.refs_3_, ...), custom_call_target="tpu_custom_call" | custom-call | flops 3221225472 | bytes 8388608 | tf_op jit(solution)/shard_map/pallas_call | solution.py:140
  95.2 4.0 %shard_map.59.refs_5_ = f32[16,3,128,128]{3,2,1,0:T(8,128)S(1)} custom-call(bf16[16,3,128,128]{3,2,1,0:T(8,128)(2,1)S(1)} %collective-permute-done.15.refs_0_, bf16[6,128,128]{2,1,0:T(8,128)(2,1)S(1)} %collective-permute-done.3.refs_1_, bf16[6,128,128]{2,1,0:T(8,128)(2,1)S(1)} %collective-permute-done.4.refs_2_, ...), custom_call_target="tpu_custom_call", output_to_operand_aliasing={{}: (5, {})} | custom-call | flops 1610612736 | bytes 8388608 | tf_op jit(solution)/shard_map/pallas_call | solution.py:140
  99.2 3.9 %shard_map.60 = bf16[16,3,128,128]{3,2,1,0:T(8,128)(2,1)S(1)} custom-call(bf16[16,3,128,128]{3,2,1,0:T(8,128)(2,1)S(1)} %collective-permute-done.15.refs_0_, bf16[6,128,128]{2,1,0:T(8,128)(2,1)S(1)} %collective-permute-done.5.refs_1_, bf16[6,128,128]{2,1,0:T(8,128)(2,1)S(1)} %collective-permute-done.6.refs_2_, ...), custom_call_target="tpu_custom_call" | custom-call | flops 1610612736 | bytes 8388608 | tf_op jit(solution)/shard_map/pallas_call | solution.py:140
  103.2 7.9 %shard_map.55.refs_5_ = f32[16,3,128,128]{3,2,1,0:T(8,128)S(1)} custom-call(bf16[16,3,128,128]{3,2,1,0:T(8,128)(2,1)S(1)} %all_to_all.10.refs_0_, bf16[6,128,128]{2,1,0:T(8,128)(2,1)S(1)} %copy-done, bf16[6,128,128]{2,1,0:T(8,128)(2,1)S(1)} %collective-permute-done.refs_2_, bf16[6,128,128]{2,1,0:T(8,128)(2,1)S(1)} %collective-permute-done.1.refs_3_, ...), custom_call_target="tpu_custom_call" | custom-call | flops 3221225472 | bytes 8388608 | tf_op jit(solution)/shard_map/pallas_call | solution.py:140
  111.1 4.0 %shard_map.56.refs_5_ = f32[16,3,128,128]{3,2,1,0:T(8,128)S(1)} custom-call(bf16[16,3,128,128]{3,2,1,0:T(8,128)(2,1)S(1)} %all_to_all.10.refs_0_, bf16[6,128,128]{2,1,0:T(8,128)(2,1)S(1)} %collective-permute-done.3.refs_1_, bf16[6,128,128]{2,1,0:T(8,128)(2,1)S(1)} %collective-permute-done.4.refs_2_, ...), custom_call_target="tpu_custom_call", output_to_operand_aliasing={{}: (5, {})} | custom-call | flops 1610612736 | bytes 8388608 | tf_op jit(solution)/shard_map/pallas_call | solution.py:140
  115.1 3.9 %shard_map.57 = bf16[16,3,128,128]{3,2,1,0:T(8,128)(2,1)S(1)} custom-call(bf16[16,3,128,128]{3,2,1,0:T(8,128)(2,1)S(1)} %all_to_all.10.refs_0_, bf16[6,128,128]{2,1,0:T(8,128)(2,1)S(1)} %collective-permute-done.5.refs_1_, bf16[6,128,128]{2,1,0:T(8,128)(2,1)S(1)} %collective-permute-done.6.refs_2_, bf16[6,128,128]{2,1,0:T(8,128)(2,1)S(1)} %collective-permute-done.13.refs_3_, ...), custom_call_target="tpu_custom_call" | custom-call | flops 1610612736 | bytes 8388608 | tf_op jit(solution)/shard_map/pallas_call | solution.py:140
  119.9 26.5 %all_to_all.11.parts_ref = bf16[16,3,128,128]{3,2,1,0:T(8,128)(2,1)S(1)} all-to-all(bf16[16,3,128,128]{3,2,1,0:T(8,128)(2,1)S(1)} %add_convert_fusion), channel_id=1, replica_groups=mesh['xh'=2,'z'=8,'xl'=2,'y'=4,'c'=2] {'xh','xl','y'}, dimensions={0} | all-to-all | bytes 3145728 | tf_op jit(solution)/shard_map/all_to_all | solution.py:201
  (18 shorter events, 1.8 us)
Async XLA Ops:
  4.6 29.7 %copy-start.1 = (bf16[6,128,128]{2,1,0:T(8,128)(2,1)S(1)}, bf16[6,128,128]{2,1,0:T(8,128)(2,1)}, u32[]{:S(2)}) copy-start(bf16[6,128,128]{2,1,0:T(8,128)(2,1)} %get-tuple-element.7.after_ref) | copy-start | bytes 589828
  4.6 31.2 %copy-start = (bf16[6,128,128]{2,1,0:T(8,128)(2,1)S(1)}, bf16[6,128,128]{2,1,0:T(8,128)(2,1)}, u32[]{:S(2)}) copy-start(bf16[6,128,128]{2,1,0:T(8,128)(2,1)} %get-tuple-element.8.refs_1_) | copy-start | bytes 589828
  34.3 52.9 %collective-permute-start.15 = (bf16[16,3,128,128]{3,2,1,0:T(8,128)(2,1)S(1)}, bf16[16,3,128,128]{3,2,1,0:T(8,128)(2,1)S(1)}, u32[]{:S(2)}, u32[]{:S(2)}) collective-permute-start(bf16[16,3,128,128]{3,2,1,0:T(8,128)(2,1)S(1)} %all_to_all.10.refs_0_), channel_id=1, source_target_pairs={{0,1},{1,0},{2,3},{3,2},{4,5},{5,4},{6,7},{7,6},{8,9},{9,8},{10,11... | collective-permute-start | bytes 4718600 | tf_op jit(solution)/shard_map/ppermute | solution.py:191
  34.3 8.5 %collective-permute-start.7 = (bf16[6,128,128]{2,1,0:T(8,128)(2,1)S(1)}, bf16[6,128,128]{2,1,0:T(8,128)(2,1)S(1)}, u32[]{:S(2)}, u32[]{:S(2)}) collective-permute-start(bf16[6,128,128]{2,1,0:T(8,128)(2,1)S(1)} %copy-done.1), channel_id=1, source_target_pairs={{0,136},{136,0},{8,128},{128,8},{1,137},{137,1},{9,129},{129,9},{2... | collective-permute-start | bytes 589832 | tf_op jit(solution)/shard_map/ppermute | solution.py:186
  35.7 10.2 %collective-permute-start = (bf16[6,128,128]{2,1,0:T(8,128)(2,1)S(1)}, bf16[6,128,128]{2,1,0:T(8,128)(2,1)S(1)}, u32[]{:S(2)}, u32[]{:S(2)}) collective-permute-start(bf16[6,128,128]{2,1,0:T(8,128)(2,1)S(1)} %copy-done), channel_id=1, source_target_pairs={{0,16},{16,32},{32,48},{48,64},{64,80},{80,96},{96,112},{112,0},{1... | collective-permute-start | bytes 589832 | tf_op jit(solution)/shard_map/ppermute | solution.py:189
  42.8 6.3 %collective-permute-start.8 = (bf16[6,128,128]{2,1,0:T(8,128)(2,1)S(1)}, bf16[6,128,128]{2,1,0:T(8,128)(2,1)S(1)}, u32[]{:S(2)}, u32[]{:S(2)}) collective-permute-start(bf16[6,128,128]{2,1,0:T(8,128)(2,1)S(1)} %collective-permute-done.7.refs_5_), channel_id=1, source_target_pairs={{0,16},{16,32},{32,48},{48,64},{64,80},{80,96},{96,112},{112,0},{1... | collective-permute-start | bytes 589832 | tf_op jit(solution)/shard_map/ppermute | solution.py:190
  45.9 6.9 %collective-permute-start.1 = (bf16[6,128,128]{2,1,0:T(8,128)(2,1)S(1)}, bf16[6,128,128]{2,1,0:T(8,128)(2,1)S(1)}, u32[]{:S(2)}, u32[]{:S(2)}) collective-permute-start(bf16[6,128,128]{2,1,0:T(8,128)(2,1)S(1)} %collective-permute-done.refs_2_), channel_id=1, source_target_pairs={{0,16},{16,32},{32,48},{48,64},{64,80},{80,96},{96,112},{112,0},{1... | collective-permute-start | bytes 589832 | tf_op jit(solution)/shard_map/ppermute | solution.py:189
  49.1 6.9 %collective-permute-start.9 = (bf16[6,128,128]{2,1,0:T(8,128)(2,1)S(1)}, bf16[6,128,128]{2,1,0:T(8,128)(2,1)S(1)}, u32[]{:S(2)}, u32[]{:S(2)}) collective-permute-start(bf16[6,128,128]{2,1,0:T(8,128)(2,1)S(1)} %collective-permute-done.8.refs_6_), channel_id=1, source_target_pairs={{0,16},{16,32},{32,48},{48,64},{64,80},{80,96},{96,112},{112,0},{1... | collective-permute-start | bytes 589832 | tf_op jit(solution)/shard_map/ppermute | solution.py:190
  52.8 6.9 %collective-permute-start.2 = (bf16[6,128,128]{2,1,0:T(8,128)(2,1)S(1)}, bf16[6,128,128]{2,1,0:T(8,128)(2,1)S(1)}, u32[]{:S(2)}, u32[]{:S(2)}) collective-permute-start(bf16[6,128,128]{2,1,0:T(8,128)(2,1)S(1)} %collective-permute-done.1.refs_3_), channel_id=1, source_target_pairs={{0,16},{16,32},{32,48},{48,64},{64,80},{80,96},{96,112},{112,0},{1... | collective-permute-start | bytes 589832 | tf_op jit(solution)/shard_map/ppermute | solution.py:189
  56.0 6.9 %collective-permute-start.10 = (bf16[6,128,128]{2,1,0:T(8,128)(2,1)S(1)}, bf16[6,128,128]{2,1,0:T(8,128)(2,1)S(1)}, u32[]{:S(2)}, u32[]{:S(2)}) collective-permute-start(bf16[6,128,128]{2,1,0:T(8,128)(2,1)S(1)} %collective-permute-done.9.refs_7_), channel_id=1, source_target_pairs={{0,16},{16,32},{32,48},{48,64},{64,80},{80,96},{96,112},{112,0},{1... | collective-permute-start | bytes 589832 | tf_op jit(solution)/shard_map/ppermute | solution.py:190
  59.7 6.9 %collective-permute-start.3 = (bf16[6,128,128]{2,1,0:T(8,128)(2,1)S(1)}, bf16[6,128,128]{2,1,0:T(8,128)(2,1)S(1)}, u32[]{:S(2)}, u32[]{:S(2)}) collective-permute-start(bf16[6,128,128]{2,1,0:T(8,128)(2,1)S(1)} %collective-permute-done.2.refs_4_), channel_id=1, source_target_pairs={{0,16},{16,32},{32,48},{48,64},{64,80},{80,96},{96,112},{112,0},{1... | collective-permute-start | bytes 589832 | tf_op jit(solution)/shard_map/ppermute | solution.py:189
  62.9 6.9 %collective-permute-start.11 = (bf16[6,128,128]{2,1,0:T(8,128)(2,1)S(1)}, bf16[6,128,128]{2,1,0:T(8,128)(2,1)S(1)}, u32[]{:S(2)}, u32[]{:S(2)}) collective-permute-start(bf16[6,128,128]{2,1,0:T(8,128)(2,1)S(1)} %collective-permute-done.10.refs_8_), channel_id=1, source_target_pairs={{0,16},{16,32},{32,48},{48,64},{64,80},{80,96},{96,112},{112,0},{1... | collective-permute-start | bytes 589832 | tf_op jit(solution)/shard_map/ppermute | solution.py:190
  66.6 6.9 %collective-permute-start.4 = (bf16[6,128,128]{2,1,0:T(8,128)(2,1)S(1)}, bf16[6,128,128]{2,1,0:T(8,128)(2,1)S(1)}, u32[]{:S(2)}, u32[]{:S(2)}) collective-permute-start(bf16[6,128,128]{2,1,0:T(8,128)(2,1)S(1)} %collective-permute-done.3.refs_1_), channel_id=1, source_target_pairs={{0,16},{16,32},{32,48},{48,64},{64,80},{80,96},{96,112},{112,0},{1... | collective-permute-start | bytes 589832 | tf_op jit(solution)/shard_map/ppermute | solution.py:189
  69.8 6.9 %collective-permute-start.12 = (bf16[6,128,128]{2,1,0:T(8,128)(2,1)S(1)}, bf16[6,128,128]{2,1,0:T(8,128)(2,1)S(1)}, u32[]{:S(2)}, u32[]{:S(2)}) collective-permute-start(bf16[6,128,128]{2,1,0:T(8,128)(2,1)S(1)} %collective-permute-done.11.refs_3_), channel_id=1, source_target_pairs={{0,16},{16,32},{32,48},{48,64},{64,80},{80,96},{96,112},{112,0},{1... | collective-permute-start | bytes 589832 | tf_op jit(solution)/shard_map/ppermute | solution.py:190
  73.5 6.9 %collective-permute-start.5 = (bf16[6,128,128]{2,1,0:T(8,128)(2,1)S(1)}, bf16[6,128,128]{2,1,0:T(8,128)(2,1)S(1)}, u32[]{:S(2)}, u32[]{:S(2)}) collective-permute-start(bf16[6,128,128]{2,1,0:T(8,128)(2,1)S(1)} %collective-permute-done.4.refs_2_), channel_id=1, source_target_pairs={{0,16},{16,32},{32,48},{48,64},{64,80},{80,96},{96,112},{112,0},{1... | collective-permute-start | bytes 589832 | tf_op jit(solution)/shard_map/ppermute | solution.py:189
  76.6 6.9 %collective-permute-start.13 = (bf16[6,128,128]{2,1,0:T(8,128)(2,1)S(1)}, bf16[6,128,128]{2,1,0:T(8,128)(2,1)S(1)}, u32[]{:S(2)}, u32[]{:S(2)}) collective-permute-start(bf16[6,128,128]{2,1,0:T(8,128)(2,1)S(1)} %collective-permute-done.12.refs_4_), channel_id=1, source_target_pairs={{0,16},{16,32},{32,48},{48,64},{64,80},{80,96},{96,112},{112,0},{1... | collective-permute-start | bytes 589832 | tf_op jit(solution)/shard_map/ppermute | solution.py:190
  80.3 18.8 %collective-permute-start.6 = (bf16[6,128,128]{2,1,0:T(8,128)(2,1)S(1)}, bf16[6,128,128]{2,1,0:T(8,128)(2,1)S(1)}, u32[]{:S(2)}, u32[]{:S(2)}) collective-permute-start(bf16[6,128,128]{2,1,0:T(8,128)(2,1)S(1)} %collective-permute-done.5.refs_1_), channel_id=1, source_target_pairs={{0,16},{16,32},{32,48},{48,64},{64,80},{80,96},{96,112},{112,0},{1... | collective-permute-start | bytes 589832 | tf_op jit(solution)/shard_map/ppermute | solution.py:189
  83.5 15.6 %collective-permute-start.14 = (bf16[6,128,128]{2,1,0:T(8,128)(2,1)S(1)}, bf16[6,128,128]{2,1,0:T(8,128)(2,1)S(1)}, u32[]{:S(2)}, u32[]{:S(2)}) collective-permute-start(bf16[6,128,128]{2,1,0:T(8,128)(2,1)S(1)} %collective-permute-done.13.refs_3_), channel_id=1, source_target_pairs={{0,16},{16,32},{32,48},{48,64},{64,80},{80,96},{96,112},{112,0},{1... | collective-permute-start | bytes 589832 | tf_op jit(solution)/shard_map/ppermute | solution.py:190
  103.1 16.0 %collective-permute-start.16 = (bf16[16,3,128,128]{3,2,1,0:T(8,128)(2,1)S(1)}, bf16[16,3,128,128]{3,2,1,0:T(8,128)(2,1)S(1)}, u32[]{:S(2)}, u32[]{:S(2)}) collective-permute-start(bf16[16,3,128,128]{3,2,1,0:T(8,128)(2,1)S(1)} %shard_map.60), channel_id=1, source_target_pairs={{0,1},{1,0},{2,3},{3,2},{4,5},{5,4},{6,7},{7,6},{8,9},{9,8},{10,11... | collective-permute-start | bytes 4718600 | tf_op jit(solution)/shard_map/ppermute | solution.py:199
